TPU v7x, 32 devices: a whole 2x2x4 slice. The times are simulated.
32 devices in a mesh: lat: 8 (over z, y), rad: 4 (over x, core).
Axes of the slice: x: 2, y: 2, z: 4, core: 2. Of those that a mesh axis runs over, the one named last changes fastest.
Arguments:
- displacement: float32 [64, 6144], P('rad', 'lat'), may hold values from -6 to 6
- surface_load: float32 [64, 6144], P('rad', 'lat'), may hold values from -6 to 6
- dens_grad: float32 [64, 6144], P('rad', 'lat'), may hold values from 0.5 to 2
- dens_ref: float32 [64], P('rad'), may hold values from 0.5 to 2
- relax_rate: float32 [64, 6144], P('rad', 'lat'), may hold values from 0.02 to 0.2
- basis: bfloat16 [2408, 6144], P(None, 'lat'), may hold values from -0.109375 to 0.109375
- neighbours: int32 [4, 6144], P(None, 'lat'), may hold values from 0 to 767
- green: float32 [49, 64, 64], replicated, may hold values from -2.5 to 2.5
Outputs:
- relaxed: float32 [64, 6144], P('rad', 'lat')
- step_sizes: float32 [3], replicated
Inputs may be any that keep to these rules, and one draw needn't show every extreme that they name: `neighbours`: indices of columns inside the same tile of 768 columns.
All inputs are finite; a program needn't handle non-finite values.
Results may differ from a plain program's by a relative error of at most 0.0045.
Values may be sent and summed in bfloat16 or wider, within the bound.
No kernel may reach another device: no remote copies, remote signals or barrier semaphores. Data moves between devices by JAX's collectives and lax.ppermute only.
A program may use at most 64 MiB of HBM per device.

v0:
```python
import jax
import jax.numpy as jnp
from jax import lax
from jax.sharding import PartitionSpec as P

DEG = 48
L = 64
ITERS = 3
KH = 2401


def extended(shard, sides, width):
    for axis, dim in sides:
        size, length = (lax.axis_size(axis), shard.shape[dim])
        up = [(i, (i + 1) % size) for i in range(size - 1)]
        down = [(j, i) for i, j in up]
        last = lax.slice_in_dim(shard, length - width, length, axis=dim)
        first = lax.slice_in_dim(shard, 0, width, axis=dim)
        before = lax.ppermute(last, axis, up)
        after = lax.ppermute(first, axis, down)
        shard = jnp.concatenate([before, shard, after], axis=dim)
    return shard


def apply_degrees(coefs, green_rows):
    blocks = []
    for degree in range(DEG + 1):
        rows = coefs[degree * degree : (degree + 1) * (degree + 1)]
        blocks.append(
            lax.dot_general(
                rows,
                green_rows[degree],
                (((1,), (1,)), ((), ())),
                precision=lax.Precision.HIGHEST,
                preferred_element_type=jnp.float32,
            )
        )
    blocks.append(jnp.zeros((coefs.shape[0] - KH, green_rows.shape[1]), jnp.float32))
    return jnp.concatenate(blocks, axis=0).astype(jnp.bfloat16)


def local(displacement, surface_load, dens_grad, dens_ref, relax_rate, basis, neighbours, green):
    u = displacement
    layers, columns = u.shape
    lat_count = lax.axis_size("lat")
    green_rows = lax.dynamic_slice_in_dim(green, lax.axis_index("rad") * layers, layers, 1)
    sizes = []
    for it in range(ITERS):
        padded = extended(u, (("rad", 0),), 1)
        rho = (dens_grad * u + dens_ref[:, None] * (padded[2:] - padded[:-2]) * 0.5).astype(
            jnp.bfloat16
        )
        partial_sums = lax.dot_general(
            basis, rho, (((1,), (1,)), ((), ())), preferred_element_type=jnp.float32
        )
        summed = lax.psum(partial_sums, "lat")
        coefs = lax.all_gather(summed, "rad", axis=1, tiled=True)
        phi = apply_degrees(coefs, green_rows)
        potential = lax.dot_general(
            phi, basis, (((0,), (0,)), ((), ())), preferred_element_type=jnp.float32
        )
        outer = extended(potential, (("rad", 0),), 1)
        force = (outer[2:] - outer[:-2]) * 0.5
        lap = jnp.sum(u[:, neighbours], axis=1) - 4.0 * u
        new = u + relax_rate * (surface_load + force + lap - u)
        squared = jnp.sum((new - u) ** 2)
        sizes.append(squared)
        u = new
    totals = jnp.stack(sizes)
    totals = lax.psum(totals, ("lat", "rad"))
    return (u, jnp.sqrt(totals / (L * columns * lat_count)))


def solution(mesh):
    placed = (
        P("rad", "lat"),
        P("rad", "lat"),
        P("rad", "lat"),
        P("rad"),
        P("rad", "lat"),
        P(None, "lat"),
        P(None, "lat"),
        P(),
    )
    return jax.shard_map(
        local, mesh=mesh, in_specs=placed, out_specs=(P("rad", "lat"), P()), check_vma=False
    )
```

profile of v0, /device:TPU:0, one launch (start us, length us, event | category | flops | bytes accessed | tf_op | source)
XLA Modules:
  0.0 424.7 jit_solution(13441633414190941219)
XLA Ops:
  8.1 2.4 collective-permute-start.1
  10.5 1.3 collective-permute-start
  11.8 3.8 collective-permute-done
  15.6 3.9 convolution_bitcast_fusion.2
  19.7 72.3 %all-reduce.4.cloned.1.call-done = f32[2408,16]{0,1:T(8,128)} async-done(((f32[2408,16]{0,1:T(8,128)}), f32[2408,16]{0,1:T(8,128)}) %all-reduce.4.cloned.1.call-update) | async-done | bytes 154128 | tf_op jit(solution)/shard_map/psum | solution.py:56
  92.0 7.9 %all_gather.9 = f32[2408,64]{0,1:T(8,128)S(1)} all-gather(f32[2408,16]{0,1:T(8,128)} %all-reduce.4.cloned.1.call-done), channel_id=1, replica_groups=mesh['lat'=8,'rad'=4] {'rad'}, dimensions={1}, use_global_device_ids=true | all-gather | bytes 770560 | tf_op jit(solution)/shard_map/all_gather | solution.py:57
  112.0 2.7 fusion.407
  114.7 2.3 collective-permute-start.3
  118.4 10.8 %gather_fusion = f32[3072,16]{1,0:T(8,128)} fusion(f32[16,768]{0,1:T(8,128)S(1)} %copy.24, s32[3072]{0:T(1024)S(1)} %broadcast_clamp_fusion), kind=kCustom, calls=%fused_computation | custom fusion | bytes 405504 | tf_op jit(solution)/shard_map/gather | solution.py:64
  129.3 1.6 reduce.3
  131.1 3.0 collective-permute-start.5
  134.1 1.3 collective-permute-start.4
  135.5 2.8 collective-permute-done.4
  138.3 3.8 convolution_bitcast_fusion.1
  142.1 70.9 %all-reduce.6.cloned.1.call-done = f32[2408,16]{0,1:T(8,128)} async-done(((f32[2408,16]{0,1:T(8,128)}), f32[2408,16]{0,1:T(8,128)}) %all-reduce.6.cloned.1.call-update) | async-done | bytes 154128 | tf_op jit(solution)/shard_map/psum | solution.py:56
  213.1 7.9 %all_gather.10 = f32[2408,64]{0,1:T(8,128)S(1)} all-gather(f32[2408,16]{0,1:T(8,128)} %all-reduce.6.cloned.1.call-done), channel_id=1, replica_groups=mesh['lat'=8,'rad'=4] {'rad'}, dimensions={1}, use_global_device_ids=true | all-gather | bytes 770560 | tf_op jit(solution)/shard_map/all_gather | solution.py:57
  233.1 2.6 fusion.408
  235.7 2.3 collective-permute-start.7
  239.4 10.8 %gather_fusion.1 = f32[3072,16]{1,0:T(8,128)} fusion(f32[16,768]{0,1:T(8,128)S(1)} %copy.34, s32[3072]{0:T(1024)S(1)} %broadcast_clamp_fusion), kind=kCustom, calls=%fused_computation.1 | custom fusion | bytes 405504 | tf_op jit(solution)/shard_map/gather | solution.py:64
  250.3 1.6 reduce.4
  252.0 3.0 collective-permute-start.9
  256.4 2.8 collective-permute-done.8
  259.2 3.8 convolution_bitcast_fusion
  263.0 71.0 %all-reduce.8.cloned.1.call-done = f32[2408,16]{0,1:T(8,128)} async-done(((f32[2408,16]{0,1:T(8,128)}), f32[2408,16]{0,1:T(8,128)}) %all-reduce.8.cloned.1.call-update) | async-done | bytes 154128 | tf_op jit(solution)/shard_map/psum | solution.py:56
  334.0 8.1 %all_gather.11 = f32[2408,64]{0,1:T(8,128)S(1)} all-gather(f32[2408,16]{0,1:T(8,128)} %all-reduce.8.cloned.1.call-done), channel_id=1, replica_groups=mesh['lat'=8,'rad'=4] {'rad'}, dimensions={1}, use_global_device_ids=true | all-gather | bytes 770560 | tf_op jit(solution)/shard_map/all_gather | solution.py:57
  354.2 2.6 fusion.409
  356.8 2.3 collective-permute-start.11
  360.6 10.8 %gather_fusion.2 = f32[3072,16]{1,0:T(8,128)} fusion(f32[16,768]{0,1:T(8,128)S(1)} %copy.44, s32[3072]{0:T(1024)S(1)} %broadcast_clamp_fusion), kind=kCustom, calls=%fused_computation.2 | custom fusion | bytes 405504 | tf_op jit(solution)/shard_map/gather | solution.py:64
  371.4 1.6 reduce.5
  373.1 1.4 multiply_reduce_fusion.2
  374.4 2.0 pad_maximum_fusion.12
  376.4 41.3 %psum.31 = f32[3]{0:T(128)S(1)} all-reduce(f32[3]{0:T(128)S(1)} %pad_maximum_fusion.12), channel_id=1, replica_groups=mesh['lat'=8,'rad'=4] {'lat','rad'}, use_global_device_ids=true, to_apply=%region_9.0 | all-reduce | flops 3 | bytes 24 | tf_op jit(solution)/shard_map/psum | solution.py:70
  (229 shorter events, 43.9 us)
Async XLA Ops:
  7.2 92.8 %copy-start = (f32[49,64,64]{2,1,0:T(8,128)S(1)}, f32[49,64,64]{2,1,0:T(8,128)}, u32[]{:S(2)}) copy-start(f32[49,64,64]{2,1,0:T(8,128)} %param.15) | copy-start | bytes 2408452
  7.2 84.8 %all-reduce.4.cloned.1.call-start = ((), (), s32[]{:S(2)}) async-start(), calls=%async_computation | async-start | bytes 311296 | tf_op jit(solution)/shard_map/psum | solution.py:56
  8.1 3.7 collective-permute-start.1
  10.5 5.2 %collective-permute-start = (f32[1,768]{1,0:T(1,128)S(1)}, f32[1,768]{1,0:T(1,128)S(1)}, u32[]{:S(2)}, u32[]{:S(2)}) collective-permute-start(f32[1,768]{1,0:T(1,128)S(1)} %get-tuple-element.16), channel_id=1, source_target_pairs={{1,0},{2,1},{3,2},{5,4},{6,5},{7,6},{9,8},{10,9},{11,10},{13,12},{... | collective-permute-start | bytes 9224 | tf_op jit(solution)/shard_map/ppermute | solution.py:20
  11.8 7.8 %copy-start.5 = (s32[4,768]{1,0:T(4,128)S(1)}, s32[4,768]{1,0:T(4,128)}, u32[]{:S(2)}) copy-start(s32[4,768]{1,0:T(4,128)} %param.14) | copy-start | bytes 36868
  19.6 193.5 %all-reduce.6.cloned.1.call-start = ((), (), s32[]{:S(2)}) async-start(), calls=%async_computation.1 | async-start | bytes 311296 | tf_op jit(solution)/shard_map/psum | solution.py:56
  112.0 6.3 %copy-start.1 = (f32[16,768]{1,0:T(8,128)S(1)}, f32[16,768]{1,0:T(8,128)}, u32[]{:S(2)}) copy-start(f32[16,768]{1,0:T(8,128)} %param.8) | copy-start | bytes 147460
  114.7 16.3 %collective-permute-start.3 = (f32[1,768]{1,0:T(1,128)S(1)}, f32[1,768]{1,0:T(1,128)S(1)}, u32[]{:S(2)}, u32[]{:S(2)}) collective-permute-start(f32[1,768]{1,0:T(1,128)S(1)} %get-tuple-element.15), channel_id=1, source_target_pairs={{0,1},{1,2},{2,3},{4,5},{5,6},{6,7},{8,9},{9,10},{10,11},{12,13},{... | collective-permute-start | bytes 9224 | tf_op jit(solution)/shard_map/ppermute | solution.py:19
  116.9 14.1 %collective-permute-start.2 = (f32[1,768]{1,0:T(1,128)S(1)}, f32[1,768]{1,0:T(1,128)S(1)}, u32[]{:S(2)}, u32[]{:S(2)}) collective-permute-start(f32[1,768]{1,0:T(1,128)S(1)} %get-tuple-element.14), channel_id=1, source_target_pairs={{1,0},{2,1},{3,2},{5,4},{6,5},{7,6},{9,8},{10,9},{11,10},{13,12},{... | collective-permute-start | bytes 9224 | tf_op jit(solution)/shard_map/ppermute | solution.py:20
  129.3 1.8 copy-start.3
  129.3 1.8 copy-start.4
  129.3 9.0 %copy-start.2 = (f32[16,768]{1,0:T(8,128)S(1)}, f32[16,768]{1,0:T(8,128)}, u32[]{:S(2)}) copy-start(f32[16,768]{1,0:T(8,128)} %param.10) | copy-start | bytes 147460
  129.3 9.0 %copy-start.6 = (f32[16]{0:T(128)S(1)}, f32[16]{0:T(128)}, u32[]{:S(2)}) copy-start(f32[16]{0:T(128)} %param.11) | copy-start | bytes 196
  131.1 4.3 %collective-permute-start.5 = (f32[1,768]{1,0:T(1,128)S(1)}, f32[1,768]{1,0:T(1,128)S(1)}, u32[]{:S(2)}, u32[]{:S(2)}) collective-permute-start(f32[1,768]{1,0:T(1,128)S(1)} %get-tuple-element.13), channel_id=1, source_target_pairs={{0,1},{1,2},{2,3},{4,5},{5,6},{6,7},{8,9},{9,10},{10,11},{12,13},{... | collective-permute-start | bytes 9224 | tf_op jit(solution)/shard_map/ppermute | solution.py:19
  134.1 4.1 collective-permute-start.4
  142.1 191.9 %all-reduce.8.cloned.1.call-start = ((), (), s32[]{:S(2)}) async-start(), calls=%async_computation.2 | async-start | bytes 311296 | tf_op jit(solution)/shard_map/psum | solution.py:56
  235.7 16.2 %collective-permute-start.7 = (f32[1,768]{1,0:T(1,128)S(1)}, f32[1,768]{1,0:T(1,128)S(1)}, u32[]{:S(2)}, u32[]{:S(2)}) collective-permute-start(f32[1,768]{1,0:T(1,128)S(1)} %get-tuple-element.11), channel_id=1, source_target_pairs={{0,1},{1,2},{2,3},{4,5},{5,6},{6,7},{8,9},{9,10},{10,11},{12,13},{... | collective-permute-start | bytes 9224 | tf_op jit(solution)/shard_map/ppermute | solution.py:19
  238.0 14.0 %collective-permute-start.6 = (f32[1,768]{1,0:T(1,128)S(1)}, f32[1,768]{1,0:T(1,128)S(1)}, u32[]{:S(2)}, u32[]{:S(2)}) collective-permute-start(f32[1,768]{1,0:T(1,128)S(1)} %get-tuple-element.10), channel_id=1, source_target_pairs={{1,0},{2,1},{3,2},{5,4},{6,5},{7,6},{9,8},{10,9},{11,10},{13,12},{... | collective-permute-start | bytes 9224 | tf_op jit(solution)/shard_map/ppermute | solution.py:20
  252.0 4.3 %collective-permute-start.9 = (f32[1,768]{1,0:T(1,128)S(1)}, f32[1,768]{1,0:T(1,128)S(1)}, u32[]{:S(2)}, u32[]{:S(2)}) collective-permute-start(f32[1,768]{1,0:T(1,128)S(1)} %get-tuple-element.9), channel_id=1, source_target_pairs={{0,1},{1,2},{2,3},{4,5},{5,6},{6,7},{8,9},{9,10},{10,11},{12,13},{... | collective-permute-start | bytes 9224 | tf_op jit(solution)/shard_map/ppermute | solution.py:19
  255.1 4.1 collective-permute-start.8
  356.8 16.2 %collective-permute-start.11 = (f32[1,768]{1,0:T(1,128)S(1)}, f32[1,768]{1,0:T(1,128)S(1)}, u32[]{:S(2)}, u32[]{:S(2)}) collective-permute-start(f32[1,768]{1,0:T(1,128)S(1)} %get-tuple-element.7), channel_id=1, source_target_pairs={{0,1},{1,2},{2,3},{4,5},{5,6},{6,7},{8,9},{9,10},{10,11},{12,13},{... | collective-permute-start | bytes 9224 | tf_op jit(solution)/shard_map/ppermute | solution.py:19
  359.1 14.0 %collective-permute-start.10 = (f32[1,768]{1,0:T(1,128)S(1)}, f32[1,768]{1,0:T(1,128)S(1)}, u32[]{:S(2)}, u32[]{:S(2)}) collective-permute-start(f32[1,768]{1,0:T(1,128)S(1)} %get-tuple-element.6), channel_id=1, source_target_pairs={{1,0},{2,1},{3,2},{5,4},{6,5},{7,6},{9,8},{10,9},{11,10},{13,12},{... | collective-permute-start | bytes 9224 | tf_op jit(solution)/shard_map/ppermute | solution.py:20
Sparse Core Ops, SparseCore 0:
  19.7 72.2 all-reduce.3
  142.2 70.8 all-reduce.5
  263.1 70.8 all-reduce.7
where the time goes:
time: 426 us; the launch traced here: 425 us
  waiting for transfers between devices  224 us (53%)
  blocking collectives  65.1 us (15%)
  matrix products  52.3 us (12%)
  local copies, waits for them, and re-layouts  37.5 us (9%)
  starting transfers between devices  23.1 us (5%)
  between operations  14.2 us (3%)
  other arithmetic  8.64 us (2%)
    psum x3, waiting for transfers between devices, local(): summed = lax.psum(partial_sums, 'lat')  214 us
    psum x1, blocking collectives, local(): totals = lax.psum(totals, ('lat', 'rad'))  41.3 us
    dot_general x147, matrix products, apply_degrees(): lax.dot_general(rows, green_rows[degree], (((1,), (1,)), ((), ())), preci...  32.9 us
    gather x3, local copies, waits for them, and re-layouts, local(): lap = jnp.sum(u[:, neighbours], axis=1) - 4.0 * u  32.5 us
    all_gather x3, blocking collectives, local(): coefs = lax.all_gather(summed, 'rad', axis=1, tiled=True)  23.9 us
    ppermute x6, starting transfers between devices, extended(): before = lax.ppermute(last, axis, up)  15.2 us
    dot_general x3, matrix products, local(): lax.dot_general(basis, rho, (((1,), (1,)), ((), ())), preferred_element_t...  11.5 us
    ppermute x6, waiting for transfers between devices, extended(): after = lax.ppermute(first, axis, down)  9.47 us
  transfers between devices with their start and end apart: 15, of which 6 were waited for; matrix products, arithmetic and copies ran while one was open for 9% of the time, Pallas kernels for 0%

commit v1 on v0

--- a/solution.py
+++ b/solution.py
@@ -53,7 +53,7 @@
         partial_sums = lax.dot_general(
             basis, rho, (((1,), (1,)), ((), ())), preferred_element_type=jnp.float32
         )
-        summed = lax.psum(partial_sums, "lat")
+        summed = jnp.sum(lax.all_gather(partial_sums, "lat"), axis=0)
         coefs = lax.all_gather(summed, "rad", axis=1, tiled=True)
         phi = apply_degrees(coefs, green_rows)
         potential = lax.dot_general(

time: 426 us -> 340 us (0.80)
  waiting for transfers between devices: 224 us -> 137 us
    psum x3 -> x0, waiting for transfers between devices: 214 us -> none  [local(): summed = lax.psum(partial_sums, 'lat')]
    all_gather x0 -> x3, waiting for transfers between devices: none -> 127 us  [local(): summed = jnp.sum(lax.all_gather(partial_sums, 'lat'), axis=0)]
  transfers between devices with their start and end apart: 15 -> 15, of which waited for: 6 -> 6; matrix products, arithmetic and copies ran while one was open for 9% -> 11% of each run, Pallas kernels for 0% -> 0%
where the time goes in v1:
time: 340 us; the launch traced here: 339 us
  waiting for transfers between devices  137 us (40%)
  blocking collectives  62.9 us (18%)
  matrix products  52.4 us (15%)
  local copies, waits for them, and re-layouts  37.5 us (11%)
  starting transfers between devices  23.1 us (7%)
  between operations  14.2 us (4%)
  other arithmetic  12.8 us (4%)
    all_gather x3, waiting for transfers between devices, local(): summed = jnp.sum(lax.all_gather(partial_sums, 'lat'), axis=0)  127 us
    psum x1, blocking collectives, local(): totals = lax.psum(totals, ('lat', 'rad'))  39.7 us
    dot_general x147, matrix products, apply_degrees(): lax.dot_general(rows, green_rows[degree], (((1,), (1,)), ((), ())), preci...  32.9 us
    gather x3, local copies, waits for them, and re-layouts, local(): lap = jnp.sum(u[:, neighbours], axis=1) - 4.0 * u  32.5 us
    all_gather x3, blocking collectives, local(): coefs = lax.all_gather(summed, 'rad', axis=1, tiled=True)  23.2 us
    ppermute x6, starting transfers between devices, extended(): before = lax.ppermute(last, axis, up)  15.2 us
    dot_general x3, matrix products, local(): lax.dot_general(basis, rho, (((1,), (1,)), ((), ())), preferred_element_t...  11.5 us
    ppermute x6, waiting for transfers between devices, extended(): after = lax.ppermute(first, axis, down)  9.49 us
  transfers between devices with their start and end apart: 15, of which 6 were waited for; matrix products, arithmetic and copies ran while one was open for 11% of the time, Pallas kernels for 0%

profile of v1, /device:TPU:0, one launch (start us, length us, event | category | flops | bytes accessed | tf_op | source)
XLA Modules:
  0.0 339.3 jit_solution(2313997748299436491)
XLA Ops:
  8.1 2.4 collective-permute-start.1
  11.8 3.8 %collective-permute-done = f32[1,768]{1,0:T(1,128)S(1)} collective-permute-done((f32[1,768]{1,0:T(1,128)S(1)}, f32[1,768]{1,0:T(1,128)S(1)}, u32[]{:S(2)}, u32[]{:S(2)}) %collective-permute-start) | collective-permute-done | bytes 3104 | tf_op jit(solution)/shard_map/ppermute | solution.py:20
  15.7 3.9 %convolution_bitcast_fusion.2 = f32[1,2408,16]{1,2,0:T(8,128)} fusion(bf16[2408,768]{1,0:T(8,128)(2,1)} %param.13, f32[16,768]{1,0:T(8,128)} %param.8, f32[1,768]{1,0:T(1,128)S(1)} %collective-permute-done.1, f32[1,768]{1,0:T(1,128)S(1)} %collective-permute-done, f32[16,768]{1,0:T(8,128)} %param.10, f32[16]{0:T(128)} %param.11), kind=kOutput, calls=%fused_computation.5 | convolution fusion | flops 59277312 | bytes 3957312 | tf_op jit(solution)/shard_map/dot_general | solution.py:53
  19.7 43.9 %all-gather.10.cloned.1.call-done = f32[8,2408,16]{1,2,0:T(8,128)} async-done(((f32[1,2408,16]{1,2,0:T(8,128)}), f32[8,2408,16]{1,2,0:T(8,128)}) %all-gather.10.cloned.1.call-update) | async-done | bytes 1232912 | tf_op jit(solution)/shard_map/all_gather | solution.py:56
  63.6 1.4 reduce_sum.81
  65.0 7.7 %all_gather.29 = f32[2408,64]{0,1:T(8,128)S(1)} all-gather(f32[2408,16]{0,1:T(8,128)S(1)} %reduce_sum.81), channel_id=1, replica_groups=mesh['lat'=8,'rad'=4] {'rad'}, dimensions={1}, use_global_device_ids=true | all-gather | bytes 770560 | tf_op jit(solution)/shard_map/all_gather | solution.py:57
  84.8 2.7 fusion.407
  87.5 2.3 collective-permute-start.3
  91.2 10.8 %gather_fusion = f32[3072,16]{1,0:T(8,128)} fusion(f32[16,768]{0,1:T(8,128)S(1)} %copy.30, s32[3072]{0:T(1024)S(1)} %broadcast_clamp_fusion), kind=kCustom, calls=%fused_computation | custom fusion | bytes 405504 | tf_op jit(solution)/shard_map/gather | solution.py:64
  102.1 1.6 reduce.3
  103.9 3.0 collective-permute-start.5
  108.3 2.8 collective-permute-done.4
  111.1 3.8 %convolution_bitcast_fusion.1 = f32[1,2408,16]{1,2,0:T(8,128)} fusion(bf16[2408,768]{1,0:T(8,128)(2,1)} %param.13, f32[16,768]{1,0:T(8,128)S(1)} %fusion.36, f32[1,768]{1,0:T(1,128)S(1)} %collective-permute-done.5, f32[1,768]{1,0:T(1,128)S(1)} %collective-permute-done.4, f32[16,768]{1,0:T(8,128)S(1)} %copy-done.2, f32[16]{0:T(128)S(1)} %copy-done.6), kind=kOutput, calls=%fused_computation.4 | convolution fusion | flops 59277312 | bytes 3957312 | tf_op jit(solution)/shard_map/dot_general | solution.py:53
  114.9 41.5 %all-gather.12.cloned.1.call-done = f32[8,2408,16]{1,2,0:T(8,128)} async-done(((f32[1,2408,16]{1,2,0:T(8,128)}), f32[8,2408,16]{1,2,0:T(8,128)}) %all-gather.12.cloned.1.call-update) | async-done | bytes 1232912 | tf_op jit(solution)/shard_map/all_gather | solution.py:56
  156.4 1.4 reduce_sum.83
  157.8 7.7 %all_gather.32 = f32[2408,64]{0,1:T(8,128)S(1)} all-gather(f32[2408,16]{0,1:T(8,128)S(1)} %reduce_sum.83), channel_id=1, replica_groups=mesh['lat'=8,'rad'=4] {'rad'}, dimensions={1}, use_global_device_ids=true | all-gather | bytes 770560 | tf_op jit(solution)/shard_map/all_gather | solution.py:57
  177.6 2.6 fusion.408
  180.2 2.3 collective-permute-start.7
  184.0 10.8 %gather_fusion.1 = f32[3072,16]{1,0:T(8,128)} fusion(f32[16,768]{0,1:T(8,128)S(1)} %copy.40, s32[3072]{0:T(1024)S(1)} %broadcast_clamp_fusion), kind=kCustom, calls=%fused_computation.1 | custom fusion | bytes 405504 | tf_op jit(solution)/shard_map/gather | solution.py:64
  194.8 1.6 reduce.4
  196.6 3.0 collective-permute-start.9
  200.9 2.8 collective-permute-done.8
  203.7 3.8 %convolution_bitcast_fusion = f32[1,2408,16]{1,2,0:T(8,128)} fusion(bf16[2408,768]{1,0:T(8,128)(2,1)} %param.13, f32[16,768]{1,0:T(8,128)S(1)} %fusion.24, f32[1,768]{1,0:T(1,128)S(1)} %collective-permute-done.9, f32[1,768]{1,0:T(1,128)S(1)} %collective-permute-done.8, f32[16,768]{1,0:T(8,128)S(1)} %copy-done.2, f32[16]{0:T(128)S(1)} %copy-done.6), kind=kOutput, calls=%fused_computation.3 | convolution fusion | flops 59277312 | bytes 3957312 | tf_op jit(solution)/shard_map/dot_general | solution.py:53
  207.5 41.5 %all-gather.14.cloned.1.call-done = f32[8,2408,16]{1,2,0:T(8,128)} async-done(((f32[1,2408,16]{1,2,0:T(8,128)}), f32[8,2408,16]{1,2,0:T(8,128)}) %all-gather.14.cloned.1.call-update) | async-done | bytes 1232912 | tf_op jit(solution)/shard_map/all_gather | solution.py:56
  249.1 1.4 reduce_sum.85
  250.4 7.9 %all_gather.35 = f32[2408,64]{0,1:T(8,128)S(1)} all-gather(f32[2408,16]{0,1:T(8,128)S(1)} %reduce_sum.85), channel_id=1, replica_groups=mesh['lat'=8,'rad'=4] {'rad'}, dimensions={1}, use_global_device_ids=true | all-gather | bytes 770560 | tf_op jit(solution)/shard_map/all_gather | solution.py:57
  270.4 2.6 fusion.409
  273.1 2.3 collective-permute-start.11
  276.8 10.8 %gather_fusion.2 = f32[3072,16]{1,0:T(8,128)} fusion(f32[16,768]{0,1:T(8,128)S(1)} %copy.50, s32[3072]{0:T(1024)S(1)} %broadcast_clamp_fusion), kind=kCustom, calls=%fused_computation.2 | custom fusion | bytes 405504 | tf_op jit(solution)/shard_map/gather | solution.py:64
  287.6 1.6 reduce.5
  290.7 2.0 pad_maximum_fusion.12
  292.6 39.7 %psum.7 = f32[3]{0:T(128)S(1)} all-reduce(f32[3]{0:T(128)S(1)} %pad_maximum_fusion.12), channel_id=1, replica_groups=mesh['lat'=8,'rad'=4] {'lat','rad'}, use_global_device_ids=true, to_apply=%region_9.0 | all-reduce | flops 3 | bytes 24 | tf_op jit(solution)/shard_map/psum | solution.py:70
  (232 shorter events, 47.9 us)
Async XLA Ops:
  7.2 65.6 %copy-start = (f32[49,64,64]{2,1,0:T(8,128)S(1)}, f32[49,64,64]{2,1,0:T(8,128)}, u32[]{:S(2)}) copy-start(f32[49,64,64]{2,1,0:T(8,128)} %param.15) | copy-start | bytes 2408452
  7.2 56.5 %all-gather.10.cloned.1.call-start = ((), (), s32[]{:S(2)}) async-start(), calls=%async_computation | async-start | bytes 1400832 | tf_op jit(solution)/shard_map/all_gather | solution.py:56
  8.1 3.7 %collective-permute-start.1 = (f32[1,768]{1,0:T(1,128)S(1)}, f32[1,768]{1,0:T(1,128)S(1)}, u32[]{:S(2)}, u32[]{:S(2)}) collective-permute-start(f32[1,768]{1,0:T(1,128)S(1)} %get-tuple-element.17), channel_id=1, source_target_pairs={{0,1},{1,2},{2,3},{4,5},{5,6},{6,7},{8,9},{9,10},{10,11},{12,13},{... | collective-permute-start | bytes 9224 | tf_op jit(solution)/shard_map/ppermute | solution.py:19
  10.5 9.2 %copy-start.5 = (s32[4,768]{1,0:T(4,128)S(1)}, s32[4,768]{1,0:T(4,128)}, u32[]{:S(2)}) copy-start(s32[4,768]{1,0:T(4,128)} %param.14) | copy-start | bytes 36868
  10.5 5.2 %collective-permute-start = (f32[1,768]{1,0:T(1,128)S(1)}, f32[1,768]{1,0:T(1,128)S(1)}, u32[]{:S(2)}, u32[]{:S(2)}) collective-permute-start(f32[1,768]{1,0:T(1,128)S(1)} %get-tuple-element.16), channel_id=1, source_target_pairs={{1,0},{2,1},{3,2},{5,4},{6,5},{7,6},{9,8},{10,9},{11,10},{13,12},{... | collective-permute-start | bytes 9224 | tf_op jit(solution)/shard_map/ppermute | solution.py:20
  19.6 136.8 %all-gather.12.cloned.1.call-start = ((), (), s32[]{:S(2)}) async-start(), calls=%async_computation.1 | async-start | bytes 1400832 | tf_op jit(solution)/shard_map/all_gather | solution.py:56
  84.8 6.3 %copy-start.1 = (f32[16,768]{1,0:T(8,128)S(1)}, f32[16,768]{1,0:T(8,128)}, u32[]{:S(2)}) copy-start(f32[16,768]{1,0:T(8,128)} %param.8) | copy-start | bytes 147460
  87.5 16.3 %collective-permute-start.3 = (f32[1,768]{1,0:T(1,128)S(1)}, f32[1,768]{1,0:T(1,128)S(1)}, u32[]{:S(2)}, u32[]{:S(2)}) collective-permute-start(f32[1,768]{1,0:T(1,128)S(1)} %get-tuple-element.15), channel_id=1, source_target_pairs={{0,1},{1,2},{2,3},{4,5},{5,6},{6,7},{8,9},{9,10},{10,11},{12,13},{... | collective-permute-start | bytes 9224 | tf_op jit(solution)/shard_map/ppermute | solution.py:19
  89.8 14.1 %collective-permute-start.2 = (f32[1,768]{1,0:T(1,128)S(1)}, f32[1,768]{1,0:T(1,128)S(1)}, u32[]{:S(2)}, u32[]{:S(2)}) collective-permute-start(f32[1,768]{1,0:T(1,128)S(1)} %get-tuple-element.14), channel_id=1, source_target_pairs={{1,0},{2,1},{3,2},{5,4},{6,5},{7,6},{9,8},{10,9},{11,10},{13,12},{... | collective-permute-start | bytes 9224 | tf_op jit(solution)/shard_map/ppermute | solution.py:20
  102.1 1.8 copy-start.3
  102.1 1.8 copy-start.4
  102.1 9.0 %copy-start.2 = (f32[16,768]{1,0:T(8,128)S(1)}, f32[16,768]{1,0:T(8,128)}, u32[]{:S(2)}) copy-start(f32[16,768]{1,0:T(8,128)} %param.10) | copy-start | bytes 147460
  102.1 9.0 %copy-start.6 = (f32[16]{0:T(128)S(1)}, f32[16]{0:T(128)}, u32[]{:S(2)}) copy-start(f32[16]{0:T(128)} %param.11) | copy-start | bytes 196
  103.9 4.3 %collective-permute-start.5 = (f32[1,768]{1,0:T(1,128)S(1)}, f32[1,768]{1,0:T(1,128)S(1)}, u32[]{:S(2)}, u32[]{:S(2)}) collective-permute-start(f32[1,768]{1,0:T(1,128)S(1)} %get-tuple-element.13), channel_id=1, source_target_pairs={{0,1},{1,2},{2,3},{4,5},{5,6},{6,7},{8,9},{9,10},{10,11},{12,13},{... | collective-permute-start | bytes 9224 | tf_op jit(solution)/shard_map/ppermute | solution.py:19
  107.0 4.1 %collective-permute-start.4 = (f32[1,768]{1,0:T(1,128)S(1)}, f32[1,768]{1,0:T(1,128)S(1)}, u32[]{:S(2)}, u32[]{:S(2)}) collective-permute-start(f32[1,768]{1,0:T(1,128)S(1)} %get-tuple-element.12), channel_id=1, source_target_pairs={{1,0},{2,1},{3,2},{5,4},{6,5},{7,6},{9,8},{10,9},{11,10},{13,12},{... | collective-permute-start | bytes 9224 | tf_op jit(solution)/shard_map/ppermute | solution.py:20
  114.9 134.2 %all-gather.14.cloned.1.call-start = ((), (), s32[]{:S(2)}) async-start(), calls=%async_computation.2 | async-start | bytes 1400832 | tf_op jit(solution)/shard_map/all_gather | solution.py:56
  180.2 16.2 %collective-permute-start.7 = (f32[1,768]{1,0:T(1,128)S(1)}, f32[1,768]{1,0:T(1,128)S(1)}, u32[]{:S(2)}, u32[]{:S(2)}) collective-permute-start(f32[1,768]{1,0:T(1,128)S(1)} %get-tuple-element.11), channel_id=1, source_target_pairs={{0,1},{1,2},{2,3},{4,5},{5,6},{6,7},{8,9},{9,10},{10,11},{12,13},{... | collective-permute-start | bytes 9224 | tf_op jit(solution)/shard_map/ppermute | solution.py:19
  182.5 14.0 %collective-permute-start.6 = (f32[1,768]{1,0:T(1,128)S(1)}, f32[1,768]{1,0:T(1,128)S(1)}, u32[]{:S(2)}, u32[]{:S(2)}) collective-permute-start(f32[1,768]{1,0:T(1,128)S(1)} %get-tuple-element.10), channel_id=1, source_target_pairs={{1,0},{2,1},{3,2},{5,4},{6,5},{7,6},{9,8},{10,9},{11,10},{13,12},{... | collective-permute-start | bytes 9224 | tf_op jit(solution)/shard_map/ppermute | solution.py:20
  196.6 4.3 %collective-permute-start.9 = (f32[1,768]{1,0:T(1,128)S(1)}, f32[1,768]{1,0:T(1,128)S(1)}, u32[]{:S(2)}, u32[]{:S(2)}) collective-permute-start(f32[1,768]{1,0:T(1,128)S(1)} %get-tuple-element.9), channel_id=1, source_target_pairs={{0,1},{1,2},{2,3},{4,5},{5,6},{6,7},{8,9},{9,10},{10,11},{12,13},{... | collective-permute-start | bytes 9224 | tf_op jit(solution)/shard_map/ppermute | solution.py:19
  199.6 4.1 %collective-permute-start.8 = (f32[1,768]{1,0:T(1,128)S(1)}, f32[1,768]{1,0:T(1,128)S(1)}, u32[]{:S(2)}, u32[]{:S(2)}) collective-permute-start(f32[1,768]{1,0:T(1,128)S(1)} %get-tuple-element.8), channel_id=1, source_target_pairs={{1,0},{2,1},{3,2},{5,4},{6,5},{7,6},{9,8},{10,9},{11,10},{13,12},{... | collective-permute-start | bytes 9224 | tf_op jit(solution)/shard_map/ppermute | solution.py:20
  273.1 16.2 %collective-permute-start.11 = (f32[1,768]{1,0:T(1,128)S(1)}, f32[1,768]{1,0:T(1,128)S(1)}, u32[]{:S(2)}, u32[]{:S(2)}) collective-permute-start(f32[1,768]{1,0:T(1,128)S(1)} %get-tuple-element.7), channel_id=1, source_target_pairs={{0,1},{1,2},{2,3},{4,5},{5,6},{6,7},{8,9},{9,10},{10,11},{12,13},{... | collective-permute-start | bytes 9224 | tf_op jit(solution)/shard_map/ppermute | solution.py:19
  275.3 14.0 %collective-permute-start.10 = (f32[1,768]{1,0:T(1,128)S(1)}, f32[1,768]{1,0:T(1,128)S(1)}, u32[]{:S(2)}, u32[]{:S(2)}) collective-permute-start(f32[1,768]{1,0:T(1,128)S(1)} %get-tuple-element.6), channel_id=1, source_target_pairs={{1,0},{2,1},{3,2},{5,4},{6,5},{7,6},{9,8},{10,9},{11,10},{13,12},{... | collective-permute-start | bytes 9224 | tf_op jit(solution)/shard_map/ppermute | solution.py:20
Sparse Core Ops, SparseCore 0:
  19.7 43.8 all-gather.9
  115.0 41.3 all-gather.11
  207.7 41.3 all-gather.13
